TPU v7x, 32 devices: a whole 2x2x4 slice. The times are simulated.
32 devices in a mesh: dp: 4 (over y, x), expert: 8 (over z, core).
Axes of the slice: x: 2, y: 2, z: 4, core: 2. Of those that a mesh axis runs over, the one named last changes fastest.
Arguments:
- hidden: bfloat16 [8, 4608, 1408], P('expert', 'dp')
- upstream: bfloat16 [8, 4608, 2048], P('expert', 'dp')
- token_counts: int32 [8, 4], P('expert', 'dp'), may hold values from 1 to 1152, as said below
- master: float32 [8, 1408, 2048], P('expert', 'dp'), may hold values from -0.15625 to 0.15625
- first_moment: float32 [8, 1408, 2048], P('expert', 'dp'), may hold values from -6 to 6
- second_moment: float32 [8, 1408, 2048], P('expert', 'dp'), may hold values from 0.25 to 4
- router_input: bfloat16 [4096, 2048], P(('dp', 'expert')), may hold values from -6 to 6
- router_cot: bfloat16 [64, 4096], P(None, ('dp', 'expert'))
- router_master: float32 [64, 2048], replicated, may hold values from -0.125 to 0.125
- router_first: float32 [64, 2048], replicated, may hold values from -6 to 6
- router_second: float32 [64, 2048], replicated, may hold values from 0.25 to 4
- partner: int32 [8], replicated, may hold values from 0 to 7, as said below
Outputs:
- new_weight: bfloat16 [8, 1408, 2048], P('expert')
- new_master: float32 [8, 1408, 2048], P('expert', 'dp')
- new_first: float32 [8, 1408, 2048], P('expert', 'dp')
- new_second: float32 [8, 1408, 2048], P('expert', 'dp')
- router_master_new: float32 [64, 2048], replicated
- router_first_new: float32 [64, 2048], replicated
- router_second_new: float32 [64, 2048], replicated
Inputs may be any that keep to these rules, and one draw needn't show every extreme that they name: partner[partner[p]] = p for every position p; a position with partner[p] = p keeps its expert. The first token_counts[e, d] of replica d's 1152 slots for position e are live, the rest are padding.
All inputs are finite; a program needn't handle non-finite values.
Results may differ from a plain program's by a relative error of at most 0.001.
Values may be sent and summed in bfloat16 or wider, within the bound.
A program may use at most 128 MiB of HBM per device.

v0:
```python
import math

import jax
import jax.numpy as jnp
from jax import lax
from jax.sharding import PartitionSpec as P

beta_first = 0.9
beta_second = 0.95
learn_rate = 0.001
decay_weight = 0.1
adam_eps = 1e-08
norm_eps = 1e-06
correct_first = 1.0 - 0.9**10
correct_second = 1.0 - 0.95**10


def adam_update(gradient, moment_one, moment_two, weights):
    first_new = beta_first * moment_one + (1.0 - beta_first) * gradient
    second_new = beta_second * moment_two + (1.0 - beta_second) * gradient * gradient
    ratio = first_new / correct_first / (jnp.sqrt(second_new / correct_second) + adam_eps)
    weights_new = weights - learn_rate * (ratio + decay_weight * weights)
    return (weights_new, first_new, second_new)


def split_pieces(matrix, groups):
    return matrix.reshape(matrix.shape[0], groups, matrix.shape[1] // groups)


def relocate_state(states, partner):
    groups = lax.axis_size("expert")
    pieces = tuple((split_pieces(member, groups) for member in states))

    def reorder(received):
        arranged = tuple((jnp.take(member, partner, axis=1) for member in received))
        return lax.all_to_all(arranged, "expert", split_axis=1, concat_axis=1, tiled=True)

    result = reorder(
        (
            lax.all_to_all(pieces[0], "expert", split_axis=1, concat_axis=1, tiled=True),
            lax.all_to_all(pieces[1], "expert", split_axis=1, concat_axis=1, tiled=True),
            lax.all_to_all(pieces[2], "expert", split_axis=1, concat_axis=1, tiled=True),
        )
    )
    return tuple((member.reshape(member.shape[0], -1) for member in result))


def regather(weight_shard):
    return lax.all_gather(weight_shard, "dp", axis=0, tiled=True)


def on_device(
    hidden,
    upstream,
    token_counts,
    master,
    first_moment,
    second_moment,
    router_input,
    router_cot,
    router_master,
    router_first,
    router_second,
    partner,
):
    hidden_units = hidden.shape[2]
    features = upstream.shape[2]
    row_count = hidden.shape[1]
    live_rows = jnp.arange(row_count, dtype=jnp.int32) < token_counts[0, 0]
    activations = hidden[0]
    grads_out = upstream[0]
    masked_out = jnp.where(live_rows[:, None], grads_out, jnp.zeros_like(grads_out))
    router_partial = jnp.dot(router_cot, router_input, preferred_element_type=jnp.float32)
    gradient = lax.psum_scatter(
        lax.dot_general(
            activations, masked_out, (((0,), (0,)), ((), ())), preferred_element_type=jnp.float32
        ),
        "dp",
        scatter_dimension=0,
        tiled=True,
    )
    router_grad, expert_square = lax.psum(
        (router_partial, jnp.sum(gradient * gradient)), ("dp", "expert")
    )
    total_square = expert_square + jnp.sum(router_grad * router_grad)
    clip_limit = 2.0 * math.sqrt(
        float(lax.axis_size("expert") * hidden_units * features + router_cot.shape[0] * features)
    )
    factor = jnp.minimum(1.0, clip_limit / (jnp.sqrt(total_square) + norm_eps))
    master_new, first_new, second_new = adam_update(
        factor * gradient, first_moment[0], second_moment[0], master[0]
    )
    router_outs = adam_update(factor * router_grad, router_first, router_second, router_master)
    moved = relocate_state((master_new, first_new, second_new), partner)
    moved_weight = regather(moved[0].astype(jnp.bfloat16))
    return (
        moved_weight[None],
        moved[0][None],
        moved[1][None],
        moved[2][None],
        router_outs[0],
        router_outs[1],
        router_outs[2],
    )


def solution(mesh):
    in_specs = (
        P("expert", "dp", None),
        P("expert", "dp", None),
        P("expert", "dp"),
        P("expert", "dp", None),
        P("expert", "dp", None),
        P("expert", "dp", None),
        P(("dp", "expert"), None),
        P(None, ("dp", "expert")),
        P(),
        P(),
        P(),
        P(),
    )
    out_specs = (
        P("expert", None, None),
        P("expert", "dp", None),
        P("expert", "dp", None),
        P("expert", "dp", None),
        P(),
        P(),
        P(),
    )
    return jax.shard_map(
        on_device, mesh=mesh, in_specs=in_specs, out_specs=out_specs, check_vma=False
    )
```

profile of v0, /device:TPU:0, one launch (start us, length us, event | category | flops | bytes accessed | tf_op | source)
XLA Modules:
  0.0 716.0 jit_solution(1665810783923439618)
XLA Ops:
  9.9 12.9 %convolution_bitcast_fusion = f32[1408,2048]{0,1:T(8,128)} fusion(bf16[1,1152,2048]{2,1,0:T(8,128)(2,1)} %param.15, pred[1152]{0:T(1024)(128)(4,1)S(1)} %iota_compare_fusion, bf16[1,1152,1408]{2,1,0:T(8,128)(2,1)S(1)} %copy-done), kind=kOutput, calls=%fused_computation.3 | convolution fusion | flops 6646136832 | bytes 19498112 | tf_op jit(solution)/shard_map/dot_general | solution.py:75
  22.8 12.0 %copy.42 = f32[1408,2048]{1,0:T(8,128)} copy(f32[1408,2048]{0,1:T(8,128)} %convolution_bitcast_fusion) | data formatting | bytes 23068672
  40.1 3.6 copy.33
  46.2 105.0 %reduce-scatter.4.cloned.1.call-done = f32[352,2048]{1,0:T(8,128)} async-done(((f32[1408,2048]{1,0:T(8,128)}), f32[352,2048]{1,0:T(8,128)}) %reduce-scatter.4.cloned.1.call-update) | async-done | bytes 2883600
  154.9 58.7 %all-reduce.2.cloned.1.call-done = f32[64,2048]{1,0:T(8,128)} async-done(((f32[64,2048]{1,0:T(8,128)}), f32[64,2048]{1,0:T(8,128)}) %all-reduce.2.cloned.1.call-update) | async-done | bytes 524304 | tf_op jit(solution)/shard_map/psum | solution.py:82
  215.4 39.5 %psum.14 = f32[]{:T(128)} all-reduce(f32[]{:T(128)} %multiply_reduce_fusion), channel_id=1, replica_groups=mesh['dp'=4,'expert'=8] {'dp','expert'}, use_global_device_ids=true, to_apply=%region_2.3 | all-reduce | flops 1 | bytes 8 | tf_op jit(solution)/shard_map/psum | solution.py:82
  256.2 6.9 bitcast_subtract_fusion
  266.6 4.7 all-to-all-start
  273.5 63.6 %all-to-all-done = f32[352,8,256]{2,0,1:T(8,128)} async-done(((f32[352,8,256]{2,0,1:T(8,128)}), f32[352,8,256]{2,0,1:T(8,128)}, u32[]{:S(2)}, u32[]{:S(2)}) %all-to-all-start) | async-done | bytes 2883616 | tf_op jit(solution)/shard_map/all_to_all | solution.py:40
  337.1 4.4 all-to-all-start.2
  343.9 63.6 %all-to-all-done.2 = f32[352,8,256]{2,0,1:T(8,128)} async-done(((f32[352,8,256]{2,0,1:T(8,128)}), f32[352,8,256]{2,0,1:T(8,128)}, u32[]{:S(2)}, u32[]{:S(2)}) %all-to-all-start.2) | async-done | bytes 2883616 | tf_op jit(solution)/shard_map/all_to_all | solution.py:41
  407.5 4.6 all-to-all-start.4
  414.7 4.1 gather_fusion.1
  418.8 59.0 %all-to-all-done.4 = f32[352,8,256]{2,0,1:T(8,128)} async-done(((f32[352,8,256]{2,0,1:T(8,128)}), f32[352,8,256]{2,0,1:T(8,128)}, u32[]{:S(2)}, u32[]{:S(2)}) %all-to-all-start.4) | async-done | bytes 2883616 | tf_op jit(solution)/shard_map/all_to_all | solution.py:42
  477.8 4.1 gather_fusion.2
  481.9 6.0 select_bitcast_fusion
  487.9 68.3 %all_to_all.30 = f32[352,8,256]{2,0,1:T(8,128)S(1)} all-to-all(f32[352,8,256]{2,0,1:T(8,128)S(1)} %get-tuple-element.16), channel_id=1, replica_groups=mesh['dp'=4,'expert'=8] {'expert'}, dimensions={1} | all-to-all | bytes 5767168 | tf_op jit(solution)/shard_map/all_to_all | solution.py:36
  556.3 4.4 all-to-all-start.3
  562.2 64.4 %all-to-all-done.3 = f32[352,8,256]{2,0,1:T(8,128)} async-done(((f32[352,8,256]{2,0,1:T(8,128)}), f32[352,8,256]{2,0,1:T(8,128)}, u32[]{:S(2)}, u32[]{:S(2)}) %all-to-all-start.3) | async-done | bytes 2883616 | tf_op jit(solution)/shard_map/all_to_all | solution.py:36
  626.6 4.5 all-to-all-start.5
  637.2 4.2 broadcast_in_dim_reshape.9
  646.7 50.3 %all-to-all-done.5 = f32[352,8,256]{2,0,1:T(8,128)} async-done(((f32[352,8,256]{2,0,1:T(8,128)}), f32[352,8,256]{2,0,1:T(8,128)}, u32[]{:S(2)}, u32[]{:S(2)}) %all-to-all-start.5) | async-done | bytes 2883616 | tf_op jit(solution)/shard_map/all_to_all | solution.py:36
  696.9 3.5 copy.41
  702.2 6.3 copy.48
  (44 shorter events, 39.7 us)
Async XLA Ops:
  8.0 1.9 copy-start
  8.0 143.1 %reduce-scatter.4.cloned.1.call-start = ((), (), s32[]{:S(2)}) async-start(), calls=%async_computation.9 | async-start | bytes 14417920
  34.8 0.7 copy-start.6
  34.8 3.0 copy-start.4
  34.8 178.7 %all-reduce.2.cloned.1.call-start = ((), (), s32[]{:S(2)}) async-start(), calls=%async_computation.7 | async-start | bytes 1048576 | tf_op jit(solution)/shard_map/psum | solution.py:82
  40.1 3.6 copy-start.5
  266.6 4.7 copy-start.3
  266.6 70.6 %all-to-all-start = ((f32[352,8,256]{2,0,1:T(8,128)}), f32[352,8,256]{2,0,1:T(8,128)}, u32[]{:S(2)}, u32[]{:S(2)}) async-start(f32[352,8,256]{2,0,1:T(8,128)} %copy.35), calls=%async_computation | async-start | bytes 5767168 | tf_op jit(solution)/shard_map/all_to_all | solution.py:40
  273.5 68.1 %copy-start.2 = (f32[352,2048]{0,1:T(8,128)S(1)}, f32[352,2048]{0,1:T(8,128)}, u32[]{:S(2)}) copy-start(f32[352,2048]{0,1:T(8,128)} %get-tuple-element.13) | copy-start | bytes 8650756
  337.1 70.3 %all-to-all-start.2 = ((f32[352,8,256]{2,0,1:T(8,128)}), f32[352,8,256]{2,0,1:T(8,128)}, u32[]{:S(2)}, u32[]{:S(2)}) async-start(f32[352,8,256]{2,0,1:T(8,128)} %copy.38), calls=%async_computation.2 | async-start | bytes 5767168 | tf_op jit(solution)/shard_map/all_to_all | solution.py:41
  343.9 68.2 %copy-start.7 = (s32[8]{0:T(128)S(1)}, s32[8]{0:T(128)}, u32[]{:S(2)}) copy-start(s32[8]{0:T(128)} %param.25) | copy-start | bytes 100
  407.5 70.3 %all-to-all-start.4 = ((f32[352,8,256]{2,0,1:T(8,128)}), f32[352,8,256]{2,0,1:T(8,128)}, u32[]{:S(2)}, u32[]{:S(2)}) async-start(f32[352,8,256]{2,0,1:T(8,128)} %copy.40), calls=%async_computation.4 | async-start | bytes 5767168 | tf_op jit(solution)/shard_map/all_to_all | solution.py:42
  556.3 70.3 %all-to-all-start.3 = ((f32[352,8,256]{2,0,1:T(8,128)}), f32[352,8,256]{2,0,1:T(8,128)}, u32[]{:S(2)}, u32[]{:S(2)}) async-start(f32[352,8,256]{2,0,1:T(8,128)} %get-tuple-element.15), calls=%async_computation.3 | async-start | bytes 5767168 | tf_op jit(solution)/shard_map/all_to_all | solution.py:36
  560.7 141.6 %all-gather.2.cloned.1.call-start = ((), (), s32[]{:S(2)}) async-start(), calls=%async_computation.8 | async-start | bytes 7208960 | tf_op jit(solution)/shard_map/all_gather | solution.py:49
  626.6 70.4 %all-to-all-start.5 = ((f32[352,8,256]{2,0,1:T(8,128)}), f32[352,8,256]{2,0,1:T(8,128)}, u32[]{:S(2)}, u32[]{:S(2)}) async-start(f32[352,8,256]{2,0,1:T(8,128)} %get-tuple-element.14), calls=%async_computation.5 | async-start | bytes 5767168 | tf_op jit(solution)/shard_map/all_to_all | solution.py:36
  702.2 6.3 copy-start.1
Sparse Core Ops, SparseCore 0:
  35.0 116.1 reduce-scatter.3
  563.9 67.7 all-gather.1
Sparse Core Ops, SparseCore 1:
  41.2 172.3 all-reduce.1
where the time goes:
time: 717 us; the launch traced here: 716 us
  waiting for transfers between devices  465 us (65%)
  blocking collectives  108 us (15%)
  local copies, waits for them, and re-layouts  68.8 us (10%)
  starting transfers between devices  22.7 us (3%)
  other arithmetic  19.2 us (3%)
  between operations  17.8 us (2%)
  matrix products  15.1 us (2%)
    all_to_all x2, waiting for transfers between devices, reorder(): lax.all_to_all(arranged, 'expert', split_axis=1, concat_axis=1, tiled=True)  115 us
    unnamed x4, waiting for transfers between devices  105 us
    all_to_all x1, blocking collectives, reorder(): lax.all_to_all(arranged, 'expert', split_axis=1, concat_axis=1, tiled=True)  68.3 us
    all_to_all x1, waiting for transfers between devices, relocate_state(): lax.all_to_all(pieces[0], 'expert', split_axis=1, concat_axis=1, tiled=True)  63.6 us
    all_to_all x1, waiting for transfers between devices, relocate_state(): lax.all_to_all(pieces[1], 'expert', split_axis=1, concat_axis=1, tiled=True)  63.6 us
    all_to_all x1, waiting for transfers between devices, relocate_state(): lax.all_to_all(pieces[2], 'expert', split_axis=1, concat_axis=1, tiled=True)  59 us
    psum x1, waiting for transfers between devices, on_device(): lax.psum((router_partial, jnp.sum(gradient * gradient)), ('dp', 'expert'))  58.7 us
    psum x1, blocking collectives, on_device(): lax.psum((router_partial, jnp.sum(gradient * gradient)), ('dp', 'expert'))  39.5 us
  transfers between devices with their start and end apart: 8, of which 7 were waited for; matrix products, arithmetic and copies ran while one was open for 7% of the time, Pallas kernels for 0%

commit v1 on v0

--- a/solution.py
+++ b/solution.py
@@ -23,26 +23,43 @@
     return (weights_new, first_new, second_new)
 
 
-def split_pieces(matrix, groups):
-    return matrix.reshape(matrix.shape[0], groups, matrix.shape[1] // groups)
+code_top = 32767.0
+steps_per_octave = 256.0
 
 
-def relocate_state(states, partner):
-    groups = lax.axis_size("expert")
-    pieces = tuple((split_pieces(member, groups) for member in states))
+def scale_of(level):
+    return jnp.exp2(level.astype(jnp.float32) * (1.0 / steps_per_octave))
 
-    def reorder(received):
-        arranged = tuple((jnp.take(member, partner, axis=1) for member in received))
-        return lax.all_to_all(arranged, "expert", split_axis=1, concat_axis=1, tiled=True)
 
-    result = reorder(
-        (
-            lax.all_to_all(pieces[0], "expert", split_axis=1, concat_axis=1, tiled=True),
-            lax.all_to_all(pieces[1], "expert", split_axis=1, concat_axis=1, tiled=True),
-            lax.all_to_all(pieces[2], "expert", split_axis=1, concat_axis=1, tiled=True),
-        )
-    )
-    return tuple((member.reshape(member.shape[0], -1) for member in result))
+def encode(blocks):
+    groups, rows, width = blocks.shape
+    peak = jnp.maximum(jnp.max(jnp.abs(blocks), axis=2), 1e-37)
+    level = jnp.clip(jnp.ceil(jnp.log2(peak) * steps_per_octave), -32000.0, 32767.0).astype(jnp.int16)
+    scaled = blocks * (code_top / scale_of(level))[:, :, None]
+    codes = jnp.clip(jnp.round(scaled), -code_top, code_top).astype(jnp.int16)
+    extra = -(-rows // width)
+    levels = jnp.pad(level, ((0, 0), (0, extra * width - rows))).reshape(groups, extra, width)
+    return jnp.concatenate([codes, levels], axis=1)
+
+
+def decode(payload, rows):
+    groups, _, width = payload.shape
+    level = payload[:, rows:].reshape(groups, -1)[:, :rows]
+    return payload[:, :rows].astype(jnp.float32) * (scale_of(level) * (1.0 / code_top))[:, :, None]
+
+
+def to_pieces(matrix, groups):
+    rows, width = matrix.shape
+    return matrix.reshape(rows, groups, width // groups).swapaxes(0, 1)
+
+
+def from_pieces(pieces):
+    groups, rows, width = pieces.shape
+    return pieces.swapaxes(0, 1).reshape(rows, groups * width)
+
+
+def exchange(payload, axis="expert"):
+    return lax.all_to_all(payload, axis, split_axis=0, concat_axis=0, tiled=True)
 
 
 def regather(weight_shard):
@@ -66,32 +83,37 @@
     hidden_units = hidden.shape[2]
     features = upstream.shape[2]
     row_count = hidden.shape[1]
+    groups = lax.axis_size("expert")
+    rows = master.shape[1]
+    early_master = exchange(encode(to_pieces(master[0], groups)))
+    early_first = exchange(encode(to_pieces(first_moment[0], groups)))
+    early_second = exchange(encode(to_pieces(second_moment[0], groups)))
     live_rows = jnp.arange(row_count, dtype=jnp.int32) < token_counts[0, 0]
     activations = hidden[0]
     grads_out = upstream[0]
     masked_out = jnp.where(live_rows[:, None], grads_out, jnp.zeros_like(grads_out))
     router_partial = jnp.dot(router_cot, router_input, preferred_element_type=jnp.float32)
-    gradient = lax.psum_scatter(
-        lax.dot_general(
-            activations, masked_out, (((0,), (0,)), ((), ())), preferred_element_type=jnp.float32
-        ),
-        "dp",
-        scatter_dimension=0,
-        tiled=True,
+    partial = lax.dot_general(
+        activations, masked_out, (((0,), (0,)), ((), ())), preferred_element_type=jnp.float32
     )
-    router_grad, expert_square = lax.psum(
-        (router_partial, jnp.sum(gradient * gradient)), ("dp", "expert")
-    )
+    gradient = lax.psum_scatter(partial, "dp", scatter_dimension=0, tiled=True)
+    moved_gradient = exchange(encode(to_pieces(gradient, groups)))
+    router_grad = lax.psum(router_partial, ("dp", "expert"))
+    expert_square = lax.psum(jnp.sum(gradient * gradient), ("dp", "expert"))
     total_square = expert_square + jnp.sum(router_grad * router_grad)
     clip_limit = 2.0 * math.sqrt(
-        float(lax.axis_size("expert") * hidden_units * features + router_cot.shape[0] * features)
+        float(groups * hidden_units * features + router_cot.shape[0] * features)
     )
     factor = jnp.minimum(1.0, clip_limit / (jnp.sqrt(total_square) + norm_eps))
-    master_new, first_new, second_new = adam_update(
-        factor * gradient, first_moment[0], second_moment[0], master[0]
+    states = adam_update(
+        factor * decode(moved_gradient, rows),
+        decode(early_first, rows),
+        decode(early_second, rows),
+        decode(early_master, rows),
     )
     router_outs = adam_update(factor * router_grad, router_first, router_second, router_master)
-    moved = relocate_state((master_new, first_new, second_new), partner)
+    sent = [encode(jnp.take(member, partner, axis=0)) for member in (states[0], states[1], states[2])]
+    moved = [from_pieces(decode(exchange(payload), rows)) for payload in sent]
     moved_weight = regather(moved[0].astype(jnp.bfloat16))
     return (
         moved_weight[None],

time: 717 us -> 546 us (0.76)
  waiting for transfers between devices: 465 us -> 281 us
  other arithmetic: 19.2 us -> 50.5 us
  blocking collectives: 108 us -> 78.9 us
    all_to_all x5 -> x6, waiting for transfers between devices: 301 us -> 117 us  [exchange(): lax.all_to_all(payload, axis, split_axis=0, concat_axis=0, tiled=True)]
    unnamed x4, waiting for transfers between devices: 105 us -> 22 us
    psum x1, waiting for transfers between devices: 58.7 us -> 141 us  [on_device(): router_grad = lax.psum(router_partial, ('dp', 'expert'))]
    all_to_all x1, blocking collectives: 68.3 us -> 39.1 us  [exchange(): lax.all_to_all(payload, axis, split_axis=0, concat_axis=0, tiled=True)]
    convert_element_type x0 -> x5, other arithmetic: none -> 11.1 us  [encode(): codes = jnp.clip(jnp.round(scaled), -code_top, code_top).astype(jnp.int16)]
    concatenate x0 -> x7, other arithmetic: none -> 10.2 us  [encode(): return jnp.concatenate([codes, levels], axis=1)]
    all_to_all x3 -> x0, local copies, waits for them, and re-layouts: 10.2 us -> none  [reorder(): lax.all_to_all(arranged, 'expert', split_axis=1, concat_axis=1, tiled=True)]
    reduce_max x0 -> x5, other arithmetic: none -> 9.97 us  [encode(): peak = jnp.maximum(jnp.max(jnp.abs(blocks), axis=2), 1e-37)]
  transfers between devices with their start and end apart: 8 -> 9, of which waited for: 7 -> 7; matrix products, arithmetic and copies ran while one was open for 7% -> 13% of each run, Pallas kernels for 0% -> 0%
where the time goes in v1:
time: 546 us; the launch traced here: 544 us
  waiting for transfers between devices  281 us (51%)
  blocking collectives  78.9 us (14%)
  local copies, waits for them, and re-layouts  72.4 us (13%)
  other arithmetic  50.5 us (9%)
  starting transfers between devices  28.2 us (5%)
  between operations  18 us (3%)
  matrix products  14.9 us (3%)
    psum x1, waiting for transfers between devices, on_device(): router_grad = lax.psum(router_partial, ('dp', 'expert'))  141 us
    all_to_all x6, waiting for transfers between devices, exchange(): lax.all_to_all(payload, axis, split_axis=0, concat_axis=0, tiled=True)  117 us
    psum x1, blocking collectives, on_device(): expert_square = lax.psum(jnp.sum(gradient * gradient), ('dp', 'expert'))  39.8 us
    all_to_all x1, blocking collectives, exchange(): lax.all_to_all(payload, axis, split_axis=0, concat_axis=0, tiled=True)  39.1 us
    unnamed x28, local copies, waits for them, and re-layouts  35.7 us
    all_to_all x6, starting transfers between devices, exchange(): lax.all_to_all(payload, axis, split_axis=0, concat_axis=0, tiled=True)  28.1 us
    unnamed x4, waiting for transfers between devices  22 us
    dot_general x1, matrix products, on_device(): lax.dot_general(activations, masked_out, (((0,), (0,)), ((), ())), prefer...  12.9 us
  transfers between devices with their start and end apart: 9, of which 7 were waited for; matrix products, arithmetic and copies ran while one was open for 13% of the time, Pallas kernels for 0%

profile of v1, /device:TPU:0, one launch (start us, length us, event | category | flops | bytes accessed | tf_op | source)
XLA Modules:
  0.0 543.5 jit_solution(693130620030949028)
XLA Ops:
  9.9 12.9 %convolution_bitcast_fusion = f32[1408,2048]{0,1:T(8,128)} fusion(bf16[1,1152,2048]{2,1,0:T(8,128)(2,1)} %param.15, pred[1152]{0:T(1024)(128)(4,1)S(1)} %iota_compare_fusion, bf16[1,1152,1408]{2,1,0:T(8,128)(2,1)S(1)} %copy-done), kind=kOutput, calls=%fused_computation.3 | convolution fusion | flops 6646136832 | bytes 19498112 | tf_op jit(solution)/shard_map/dot_general | solution.py:96
  22.8 12.0 %copy.42 = f32[1408,2048]{1,0:T(8,128)} copy(f32[1408,2048]{0,1:T(8,128)} %convolution_bitcast_fusion) | data formatting | bytes 23068672
  41.4 6.4 %all-to-all-start.3 = ((s16[8,354,256]{2,1,0:T(8,128)(2,1)}), s16[8,354,256]{2,1,0:T(8,128)(2,1)}, u32[]{:S(2)}, u32[]{:S(2)}) async-start(s16[8,354,256]{2,1,0:T(8,128)(2,1)} %pad_add_fusion.3), calls=%async_computation.3 | async-start | bytes 2949120 | tf_op jit(solution)/shard_map/all_to_all | solution.py:62
  54.2 29.3 %all-to-all-done.3 = s16[8,354,256]{2,1,0:T(8,128)(2,1)} async-done(((s16[8,354,256]{2,1,0:T(8,128)(2,1)}), s16[8,354,256]{2,1,0:T(8,128)(2,1)}, u32[]{:S(2)}, u32[]{:S(2)}) %all-to-all-start.3) | async-done | bytes 1450016 | tf_op jit(solution)/shard_map/all_to_all | solution.py:62
  83.5 4.3 all-to-all-start.1
  94.3 29.2 %all-to-all-done.1 = s16[8,354,256]{2,1,0:T(8,128)(2,1)} async-done(((s16[8,354,256]{2,1,0:T(8,128)(2,1)}), s16[8,354,256]{2,1,0:T(8,128)(2,1)}, u32[]{:S(2)}, u32[]{:S(2)}) %all-to-all-start.1) | async-done | bytes 1450016 | tf_op jit(solution)/shard_map/all_to_all | solution.py:62
  123.5 4.3 all-to-all-start
  127.8 22.0 %reduce-scatter.4.cloned.1.call-done = f32[352,2048]{1,0:T(8,128)} async-done(((f32[1408,2048]{1,0:T(8,128)}), f32[352,2048]{1,0:T(8,128)}) %reduce-scatter.4.cloned.1.call-update) | async-done | bytes 2883600
  163.5 4.3 all-to-all-start.2
  170.0 141.4 %all-reduce.9.cloned.1.call-done = f32[64,2048]{1,0:T(8,128)} async-done(((f32[64,2048]{1,0:T(8,128)}), f32[64,2048]{1,0:T(8,128)}) %all-reduce.9.cloned.1.call-update) | async-done | bytes 524304 | tf_op jit(solution)/shard_map/psum | solution.py:101
  317.0 39.8 %psum.14 = f32[]{:T(128)} all-reduce(f32[]{:T(128)} %multiply_reduce_fusion), channel_id=1, replica_groups=mesh['dp'=4,'expert'=8] {'dp','expert'}, use_global_device_ids=true, to_apply=%region_4.5 | all-reduce | flops 1 | bytes 8 | tf_op jit(solution)/shard_map/psum | solution.py:102
  358.9 8.5 %multiply_subtract_fusion = (f32[8,352,256]{2,1,0:T(8,128)}, f32[8,352,256]{2,1,0:T(8,128)}, f32[8,352,256]{2,1,0:T(8,128)}) fusion(s16[8,354,256]{2,1,0:T(8,128)(2,1)} %all-to-all-done, f32[8,352]{1,0:T(8,128)S(1)} %exponential_multiply_fusion.6, f32[8,352]{1,0:T(8,128)S(1)} %exponential_multiply_fusion.4, s16[8,354,256]{2,1,0:T(8,128)(2,1)} %all-to-all-done.2, ...), kind=kLoop, calls=%fused_computation.44 | loop fusion | flops 17301504 | bytes 14462980 | tf_op jit(solution)/shard_map/sub | solution.py:22
  370.0 4.1 gather_fusion.1
  378.2 4.4 abs_reduce_fusion
  382.8 5.7 %clamp_convert_fusion = (s16[8,352,256]{2,1,0:T(8,128)(2,1)}, s16[8,352,256]{2,1,0:T(8,128)(2,1)}, s16[8,352,256]{2,1,0:T(8,128)(2,1)S(1)}) fusion(f32[8,352,256]{2,1,0:T(8,128)} %gather_fusion.2, f32[8,352]{1,0:T(8,128)S(1)} %get-tuple-element.14, pred[8]{0:T(512)(128)(4,1)S(1)} %compare_and_fusion, f32[8,352]{1,0:T(8,128)S(1)} %get-tuple-element.36, ...), kind=kLoop, calls=%fused_computation.36 | loop fusion | flops 10813440 | bytes 13009928 | tf_op jit(solution)/shard_map/convert_element_type | solution.py:39
  388.6 39.1 %all_to_all.35 = s16[8,354,256]{2,1,0:T(8,128)(2,1)S(1)} all-to-all(s16[8,354,256]{2,1,0:T(8,128)(2,1)S(1)} %pad_add_fusion.4), channel_id=1, replica_groups=mesh['dp'=4,'expert'=8] {'expert'}, dimensions={0} | all-to-all | bytes 2899968 | tf_op jit(solution)/shard_map/all_to_all | solution.py:62
  432.2 4.3 all-to-all-start.6
  439.3 32.9 %all-to-all-done.6 = s16[8,354,256]{2,1,0:T(8,128)(2,1)} async-done(((s16[8,354,256]{2,1,0:T(8,128)(2,1)}), s16[8,354,256]{2,1,0:T(8,128)(2,1)}, u32[]{:S(2)}, u32[]{:S(2)}) %all-to-all-start.6) | async-done | bytes 1450016 | tf_op jit(solution)/shard_map/all_to_all | solution.py:62
  472.3 4.6 all-to-all-start.5
  485.7 4.2 broadcast_in_dim_reshape.11
  489.8 22.4 %all-to-all-done.5 = s16[8,354,256]{2,1,0:T(8,128)(2,1)} async-done(((s16[8,354,256]{2,1,0:T(8,128)(2,1)}), s16[8,354,256]{2,1,0:T(8,128)(2,1)}, u32[]{:S(2)}, u32[]{:S(2)}) %all-to-all-start.5) | async-done | bytes 1450016 | tf_op jit(solution)/shard_map/all_to_all | solution.py:62
  518.2 4.2 broadcast_in_dim_reshape.10
  525.6 4.2 broadcast_in_dim_reshape.9
  529.8 6.3 %copy.64 = bf16[1,1408,2048]{2,1,0:T(8,128)(2,1)} copy(bf16[1,1408,2048]{2,1,0:T(8,128)(2,1)} %bitcast.107) | data formatting | bytes 11534336
  (95 shorter events, 74.9 us)
Async XLA Ops:
  8.0 1.9 copy-start
  8.0 141.7 %reduce-scatter.4.cloned.1.call-start = ((), (), s32[]{:S(2)}) async-start(), calls=%async_computation.10 | async-start | bytes 14417920
  41.4 42.2 %all-to-all-start.3 = ((s16[8,354,256]{2,1,0:T(8,128)(2,1)}), s16[8,354,256]{2,1,0:T(8,128)(2,1)}, u32[]{:S(2)}, u32[]{:S(2)}) async-start(s16[8,354,256]{2,1,0:T(8,128)(2,1)} %pad_add_fusion.3), calls=%async_computation.3 | async-start | bytes 2949120 | tf_op jit(solution)/shard_map/all_to_all | solution.py:62
  83.5 40.0 %all-to-all-start.1 = ((s16[8,354,256]{2,1,0:T(8,128)(2,1)}), s16[8,354,256]{2,1,0:T(8,128)(2,1)}, u32[]{:S(2)}, u32[]{:S(2)}) async-start(s16[8,354,256]{2,1,0:T(8,128)(2,1)} %pad_add_fusion.1), calls=%async_computation.1 | async-start | bytes 2949120 | tf_op jit(solution)/shard_map/all_to_all | solution.py:62
  123.5 40.0 %all-to-all-start = ((s16[8,354,256]{2,1,0:T(8,128)(2,1)}), s16[8,354,256]{2,1,0:T(8,128)(2,1)}, u32[]{:S(2)}, u32[]{:S(2)}) async-start(s16[8,354,256]{2,1,0:T(8,128)(2,1)} %pad_add_fusion), calls=%async_computation | async-start | bytes 2949120 | tf_op jit(solution)/shard_map/all_to_all | solution.py:62
  159.0 8.8 %copy-start.2 = (bf16[64,128]{1,0:T(8,128)(2,1)S(1)}, bf16[64,128]{1,0:T(8,128)(2,1)}, u32[]{:S(2)}) copy-start(bf16[64,128]{1,0:T(8,128)(2,1)} %param.21) | copy-start | bytes 49156
  160.2 9.8 %copy-start.3 = (s32[8]{0:T(128)S(1)}, s32[8]{0:T(128)}, u32[]{:S(2)}) copy-start(s32[8]{0:T(128)} %param.25) | copy-start | bytes 100
  163.5 194.7 %all-to-all-start.2 = ((s16[8,354,256]{2,1,0:T(8,128)(2,1)}), s16[8,354,256]{2,1,0:T(8,128)(2,1)}, u32[]{:S(2)}, u32[]{:S(2)}) async-start(s16[8,354,256]{2,1,0:T(8,128)(2,1)} %pad_add_fusion.2), calls=%async_computation.2 | async-start | bytes 2949120 | tf_op jit(solution)/shard_map/all_to_all | solution.py:62
  167.8 143.6 %all-reduce.9.cloned.1.call-start = ((), (), s32[]{:S(2)}) async-start(), calls=%async_computation.8 | async-start | bytes 1048576 | tf_op jit(solution)/shard_map/psum | solution.py:101
  169.9 359.8 %all-gather.2.cloned.1.call-start = ((), (), s32[]{:S(2)}) async-start(), calls=%async_computation.9 | async-start | bytes 7208960 | tf_op jit(solution)/shard_map/all_gather | solution.py:66
  432.2 40.0 %all-to-all-start.6 = ((s16[8,354,256]{2,1,0:T(8,128)(2,1)}), s16[8,354,256]{2,1,0:T(8,128)(2,1)}, u32[]{:S(2)}, u32[]{:S(2)}) async-start(s16[8,354,256]{2,1,0:T(8,128)(2,1)} %pad_add_fusion.6), calls=%async_computation.6 | async-start | bytes 2949120 | tf_op jit(solution)/shard_map/all_to_all | solution.py:62
  472.3 40.0 %all-to-all-start.5 = ((s16[8,354,256]{2,1,0:T(8,128)(2,1)}), s16[8,354,256]{2,1,0:T(8,128)(2,1)}, u32[]{:S(2)}, u32[]{:S(2)}) async-start(s16[8,354,256]{2,1,0:T(8,128)(2,1)} %pad_add_fusion.5), calls=%async_computation.5 | async-start | bytes 2949120 | tf_op jit(solution)/shard_map/all_to_all | solution.py:62
  529.8 6.3 %copy-start.1 = (bf16[1,1152,1408]{2,1,0:T(8,128)(2,1)S(1)}, bf16[1,1152,1408]{2,1,0:T(8,128)(2,1)}, u32[]{:S(2)}) copy-start(bf16[1,1152,1408]{2,1,0:T(8,128)(2,1)} %param.14) | copy-start | bytes 9732100
Sparse Core Ops, SparseCore 0:
  35.0 114.7 reduce-scatter.3
  429.8 64.6 all-gather.1
Sparse Core Ops, SparseCore 1:
  174.1 137.3 all-reduce.8

commit v2 on v1

--- a/solution.py
+++ b/solution.py
@@ -93,14 +93,20 @@
     grads_out = upstream[0]
     masked_out = jnp.where(live_rows[:, None], grads_out, jnp.zeros_like(grads_out))
     router_partial = jnp.dot(router_cot, router_input, preferred_element_type=jnp.float32)
+    everyone = lax.axis_size("dp") * groups
+    router_terms = exchange(router_partial.reshape(everyone, -1), ("dp", "expert"))
+    router_share = jnp.sum(router_terms, axis=0)
     partial = lax.dot_general(
         activations, masked_out, (((0,), (0,)), ((), ())), preferred_element_type=jnp.float32
     )
     gradient = lax.psum_scatter(partial, "dp", scatter_dimension=0, tiled=True)
     moved_gradient = exchange(encode(to_pieces(gradient, groups)))
-    router_grad = lax.psum(router_partial, ("dp", "expert"))
-    expert_square = lax.psum(jnp.sum(gradient * gradient), ("dp", "expert"))
-    total_square = expert_square + jnp.sum(router_grad * router_grad)
+    packet = jnp.concatenate(
+        [router_share, jnp.full((128,), jnp.sum(gradient * gradient), jnp.float32)]
+    )
+    packets = lax.all_gather(packet, ("dp", "expert"), axis=0)
+    router_grad = packets[:, : router_share.shape[0]].reshape(router_partial.shape)
+    total_square = jnp.sum(packets[:, -1]) + jnp.sum(router_grad * router_grad)
     clip_limit = 2.0 * math.sqrt(
         float(groups * hidden_units * features + router_cot.shape[0] * features)
     )

time: 546 us -> 441 us (0.81)
  waiting for transfers between devices: 281 us -> 145 us
  blocking collectives: 78.9 us -> 99.7 us
  starting transfers between devices: 28.2 us -> 33.8 us
    psum x1 -> x0, waiting for transfers between devices: 141 us -> none  [on_device(): router_grad = lax.psum(router_partial, ('dp', 'expert'))]
    all_gather x0 -> x1, blocking collectives: none -> 61.6 us  [on_device(): packets = lax.all_gather(packet, ('dp', 'expert'), axis=0)]
    psum x1 -> x0, blocking collectives: 39.8 us -> none  [on_device(): expert_square = lax.psum(jnp.sum(gradient * gradient), ('dp', 'expert'))]
    all_to_all x6 -> x7, waiting for transfers between devices: 117 us -> 135 us  [exchange(): lax.all_to_all(payload, axis, split_axis=0, concat_axis=0, tiled=True)]
    unnamed x4 -> x3, waiting for transfers between devices: 22 us -> 9.81 us
    all_to_all x6 -> x7, starting transfers between devices: 28.1 us -> 33.7 us  [exchange(): lax.all_to_all(payload, axis, split_axis=0, concat_axis=0, tiled=True)]
    unnamed x28 -> x34, local copies, waits for them, and re-layouts: 35.7 us -> 36.8 us
  transfers between devices with their start and end apart: 9 -> 9, of which waited for: 7 -> 7; matrix products, arithmetic and copies ran while one was open for 13% -> 18% of each run, Pallas kernels for 0% -> 0%
where the time goes in v2:
time: 441 us; the launch traced here: 439 us
  waiting for transfers between devices  145 us (33%)
  blocking collectives  99.7 us (23%)
  local copies, waits for them, and re-layouts  77.5 us (18%)
  other arithmetic  53.3 us (12%)
  starting transfers between devices  33.8 us (8%)
  between operations  16.6 us (4%)
  matrix products  13.1 us (3%)
    all_to_all x7, waiting for transfers between devices, exchange(): lax.all_to_all(payload, axis, split_axis=0, concat_axis=0, tiled=True)  135 us
    all_gather x1, blocking collectives, on_device(): packets = lax.all_gather(packet, ('dp', 'expert'), axis=0)  61.6 us
    all_to_all x1, blocking collectives, exchange(): lax.all_to_all(payload, axis, split_axis=0, concat_axis=0, tiled=True)  38.1 us
    unnamed x34, local copies, waits for them, and re-layouts  36.8 us
    all_to_all x7, starting transfers between devices, exchange(): lax.all_to_all(payload, axis, split_axis=0, concat_axis=0, tiled=True)  33.7 us
    dot_general x1, matrix products, on_device(): lax.dot_general(activations, masked_out, (((0,), (0,)), ((), ())), prefer...  12.9 us
    sub x2, other arithmetic, adam_update(): weights_new = weights - learn_rate * (ratio + decay_weight * weights)  11.4 us
    convert_element_type x5, other arithmetic, encode(): codes = jnp.clip(jnp.round(scaled), -code_top, code_top).astype(jnp.int16)  11.1 us
  transfers between devices with their start and end apart: 9, of which 7 were waited for; matrix products, arithmetic and copies ran while one was open for 18% of the time, Pallas kernels for 0%

profile of v2, /device:TPU:0, one launch (start us, length us, event | category | flops | bytes accessed | tf_op | source)
XLA Modules:
  0.0 438.9 jit_solution(546738193907587709)
XLA Ops:
  9.1 12.9 %convolution_bitcast_fusion = f32[1408,2048]{0,1:T(8,128)} fusion(bf16[1,1152,2048]{2,1,0:T(8,128)(2,1)} %param.15, pred[1152]{0:T(1024)(128)(4,1)S(1)} %iota_compare_fusion, bf16[1,1152,1408]{2,1,0:T(8,128)(2,1)S(1)} %copy-done), kind=kOutput, calls=%fused_computation.3 | convolution fusion | flops 6646136832 | bytes 19498112 | tf_op jit(solution)/shard_map/dot_general | solution.py:99
  22.0 12.0 %copy.43 = f32[1408,2048]{1,0:T(8,128)} copy(f32[1408,2048]{0,1:T(8,128)} %convolution_bitcast_fusion) | data formatting | bytes 23068672
  36.6 7.5 %all-to-all-start.2 = ((f32[32,1,4096]{2,1,0:T(1,128)}), f32[32,1,4096]{2,1,0:T(1,128)}, u32[]{:S(2)}, u32[]{:S(2)}) async-start(f32[32,1,4096]{2,1,0:T(1,128)} %all_to_all.36), calls=%async_computation.2 | async-start | bytes 1048576 | tf_op jit(solution)/shard_map/all_to_all | solution.py:62
  50.6 9.8 %all-to-all-done.2 = f32[32,1,4096]{2,1,0:T(1,128)} async-done(((f32[32,1,4096]{2,1,0:T(1,128)}), f32[32,1,4096]{2,1,0:T(1,128)}, u32[]{:S(2)}, u32[]{:S(2)}) %all-to-all-start.2) | async-done | bytes 524320 | tf_op jit(solution)/shard_map/all_to_all | solution.py:62
  60.4 4.5 %all-to-all-start.4 = ((s16[8,354,256]{2,1,0:T(8,128)(2,1)}), s16[8,354,256]{2,1,0:T(8,128)(2,1)}, u32[]{:S(2)}, u32[]{:S(2)}) async-start(s16[8,354,256]{2,1,0:T(8,128)(2,1)} %pad_add_fusion.3), calls=%async_computation.4 | async-start | bytes 2949120 | tf_op jit(solution)/shard_map/all_to_all | solution.py:62
  71.4 29.0 %all-to-all-done.4 = s16[8,354,256]{2,1,0:T(8,128)(2,1)} async-done(((s16[8,354,256]{2,1,0:T(8,128)(2,1)}), s16[8,354,256]{2,1,0:T(8,128)(2,1)}, u32[]{:S(2)}, u32[]{:S(2)}) %all-to-all-start.4) | async-done | bytes 1450016 | tf_op jit(solution)/shard_map/all_to_all | solution.py:62
  100.4 4.3 all-to-all-start.1
  111.2 29.2 %all-to-all-done.1 = s16[8,354,256]{2,1,0:T(8,128)(2,1)} async-done(((s16[8,354,256]{2,1,0:T(8,128)(2,1)}), s16[8,354,256]{2,1,0:T(8,128)(2,1)}, u32[]{:S(2)}, u32[]{:S(2)}) %all-to-all-start.1) | async-done | bytes 1450016 | tf_op jit(solution)/shard_map/all_to_all | solution.py:62
  140.4 4.3 all-to-all-start
  144.7 9.8 %reduce-scatter.4.cloned.1.call-done = f32[352,2048]{1,0:T(8,128)} async-done(((f32[1408,2048]{1,0:T(8,128)}), f32[352,2048]{1,0:T(8,128)}) %reduce-scatter.4.cloned.1.call-update) | async-done | bytes 2883600
  165.0 15.5 %all-to-all-done = s16[8,354,256]{2,1,0:T(8,128)(2,1)} async-done(((s16[8,354,256]{2,1,0:T(8,128)(2,1)}), s16[8,354,256]{2,1,0:T(8,128)(2,1)}, u32[]{:S(2)}, u32[]{:S(2)}) %all-to-all-start) | async-done | bytes 1450016 | tf_op jit(solution)/shard_map/all_to_all | solution.py:62
  180.4 4.3 all-to-all-start.3
  190.7 61.6 %all-gather.1 = f32[32,1,4224]{2,1,0:T(1,128)S(1)} all-gather(f32[1,1,4224]{2,1,0:T(1,128)S(1)} %reshape.219), channel_id=2, replica_groups=mesh['dp'=4,'expert'=8] {'dp','expert'}, dimensions={0}, use_global_device_ids=true | all-gather | bytes 557568 | tf_op jit(solution)/shard_map/all_gather | solution.py:107
  255.9 8.5 %multiply_subtract_fusion = (f32[8,352,256]{2,1,0:T(8,128)}, f32[8,352,256]{2,1,0:T(8,128)}, f32[8,352,256]{2,1,0:T(8,128)}) fusion(s16[8,354,256]{2,1,0:T(8,128)(2,1)} %all-to-all-done, f32[8,352]{1,0:T(8,128)S(1)} %exponential_multiply_fusion.6, f32[8,352]{1,0:T(8,128)S(1)} %exponential_multiply_fusion.4, s16[8,354,256]{2,1,0:T(8,128)(2,1)} %all-to-all-done.3, ...), kind=kLoop, calls=%fused_computation.44 | loop fusion | flops 17301504 | bytes 14462980 | tf_op jit(solution)/shard_map/sub | solution.py:22
  275.2 4.4 %abs_reduce_fusion = (f32[8,352]{1,0:T(8,128)S(1)}, f32[8,352]{1,0:T(8,128)S(1)}, f32[8,352]{1,0:T(8,128)S(1)}) fusion(f32[8,352,256]{2,1,0:T(8,128)} %gather_fusion.2, pred[8]{0:T(512)(128)(4,1)S(1)} %compare_and_fusion, f32[8,352,256]{2,1,0:T(8,128)} %gather_fusion.1, f32[8,352,256]{2,1,0:T(8,128)S(1)} %gather_fusion), kind=kLoop, calls=%fused_computation.37 | loop fusion | flops 6479616 | bytes 8684552 | tf_op jit(solution)/shard_map/reduce_max | solution.py:36
  279.8 5.7 %clamp_convert_fusion = (s16[8,352,256]{2,1,0:T(8,128)(2,1)}, s16[8,352,256]{2,1,0:T(8,128)(2,1)}, s16[8,352,256]{2,1,0:T(8,128)(2,1)S(1)}) fusion(f32[8,352,256]{2,1,0:T(8,128)} %gather_fusion.2, f32[8,352]{1,0:T(8,128)S(1)} %get-tuple-element.14, pred[8]{0:T(512)(128)(4,1)S(1)} %compare_and_fusion, f32[8,352]{1,0:T(8,128)S(1)} %get-tuple-element.36, ...), kind=kLoop, calls=%fused_computation.36 | loop fusion | flops 10813440 | bytes 13009928 | tf_op jit(solution)/shard_map/convert_element_type | solution.py:39
  285.5 38.1 %all_to_all.45 = s16[8,354,256]{2,1,0:T(8,128)(2,1)S(1)} all-to-all(s16[8,354,256]{2,1,0:T(8,128)(2,1)S(1)} %pad_add_fusion.4), channel_id=1, replica_groups=mesh['dp'=4,'expert'=8] {'expert'}, dimensions={0} | all-to-all | bytes 2899968 | tf_op jit(solution)/shard_map/all_to_all | solution.py:62
  328.2 4.4 all-to-all-start.7
  335.3 33.0 %all-to-all-done.7 = s16[8,354,256]{2,1,0:T(8,128)(2,1)} async-done(((s16[8,354,256]{2,1,0:T(8,128)(2,1)}), s16[8,354,256]{2,1,0:T(8,128)(2,1)}, u32[]{:S(2)}, u32[]{:S(2)}) %all-to-all-start.7) | async-done | bytes 1450016 | tf_op jit(solution)/shard_map/all_to_all | solution.py:62
  368.3 4.6 %all-to-all-start.6 = ((s16[8,354,256]{2,1,0:T(8,128)(2,1)}), s16[8,354,256]{2,1,0:T(8,128)(2,1)}, u32[]{:S(2)}, u32[]{:S(2)}) async-start(s16[8,354,256]{2,1,0:T(8,128)(2,1)} %pad_add_fusion.5), calls=%async_computation.6 | async-start | bytes 2949120 | tf_op jit(solution)/shard_map/all_to_all | solution.py:62
  385.4 4.2 broadcast_in_dim_reshape.11
  389.6 18.7 %all-to-all-done.6 = s16[8,354,256]{2,1,0:T(8,128)(2,1)} async-done(((s16[8,354,256]{2,1,0:T(8,128)(2,1)}), s16[8,354,256]{2,1,0:T(8,128)(2,1)}, u32[]{:S(2)}, u32[]{:S(2)}) %all-to-all-start.6) | async-done | bytes 1450016 | tf_op jit(solution)/shard_map/all_to_all | solution.py:62
  414.2 4.2 broadcast_in_dim_reshape.10
  425.8 6.3 %copy.67 = bf16[1,1408,2048]{2,1,0:T(8,128)(2,1)} copy(bf16[1,1408,2048]{2,1,0:T(8,128)(2,1)} %bitcast.110) | data formatting | bytes 11534336
  (106 shorter events, 85.9 us)
Async XLA Ops:
  7.2 1.9 copy-start
  7.2 147.3 %reduce-scatter.4.cloned.1.call-start = ((), (), s32[]{:S(2)}) async-start(), calls=%async_computation.10 | async-start | bytes 14417920
  34.0 1.0 copy-start.3
  34.0 1.0 copy-start.4
  36.6 23.8 %all-to-all-start.2 = ((f32[32,1,4096]{2,1,0:T(1,128)}), f32[32,1,4096]{2,1,0:T(1,128)}, u32[]{:S(2)}, u32[]{:S(2)}) async-start(f32[32,1,4096]{2,1,0:T(1,128)} %all_to_all.36), calls=%async_computation.2 | async-start | bytes 1048576 | tf_op jit(solution)/shard_map/all_to_all | solution.py:62
  60.4 40.0 %all-to-all-start.4 = ((s16[8,354,256]{2,1,0:T(8,128)(2,1)}), s16[8,354,256]{2,1,0:T(8,128)(2,1)}, u32[]{:S(2)}, u32[]{:S(2)}) async-start(s16[8,354,256]{2,1,0:T(8,128)(2,1)} %pad_add_fusion.3), calls=%async_computation.4 | async-start | bytes 2949120 | tf_op jit(solution)/shard_map/all_to_all | solution.py:62
  100.4 40.0 %all-to-all-start.1 = ((s16[8,354,256]{2,1,0:T(8,128)(2,1)}), s16[8,354,256]{2,1,0:T(8,128)(2,1)}, u32[]{:S(2)}, u32[]{:S(2)}) async-start(s16[8,354,256]{2,1,0:T(8,128)(2,1)} %pad_add_fusion.1), calls=%async_computation.1 | async-start | bytes 2949120 | tf_op jit(solution)/shard_map/all_to_all | solution.py:62
  140.4 40.0 %all-to-all-start = ((s16[8,354,256]{2,1,0:T(8,128)(2,1)}), s16[8,354,256]{2,1,0:T(8,128)(2,1)}, u32[]{:S(2)}, u32[]{:S(2)}) async-start(s16[8,354,256]{2,1,0:T(8,128)(2,1)} %pad_add_fusion), calls=%async_computation | async-start | bytes 2949120 | tf_op jit(solution)/shard_map/all_to_all | solution.py:62
  163.8 21.0 %copy-start.5 = (s32[8]{0:T(128)S(1)}, s32[8]{0:T(128)}, u32[]{:S(2)}) copy-start(s32[8]{0:T(128)} %param.25) | copy-start | bytes 100
  180.4 74.7 %all-to-all-start.3 = ((s16[8,354,256]{2,1,0:T(8,128)(2,1)}), s16[8,354,256]{2,1,0:T(8,128)(2,1)}, u32[]{:S(2)}, u32[]{:S(2)}) async-start(s16[8,354,256]{2,1,0:T(8,128)(2,1)} %pad_add_fusion.2), calls=%async_computation.3 | async-start | bytes 2949120 | tf_op jit(solution)/shard_map/all_to_all | solution.py:62
  184.7 241.0 %all-gather.4.cloned.1.call-start = ((), (), s32[]{:S(2)}) async-start(), calls=%async_computation.9 | async-start | bytes 7208960 | tf_op jit(solution)/shard_map/all_gather | solution.py:66
  252.3 12.1 %copy-start.2 = (f32[32,1,4224]{2,0,1:T(8,128)}, f32[32,1,4224]{2,0,1:T(8,128)S(1)}, u32[]{:S(2)}) copy-start(f32[32,1,4224]{2,0,1:T(8,128)S(1)} %copy.64) | copy-start | bytes 1622020
  328.2 40.1 %all-to-all-start.7 = ((s16[8,354,256]{2,1,0:T(8,128)(2,1)}), s16[8,354,256]{2,1,0:T(8,128)(2,1)}, u32[]{:S(2)}, u32[]{:S(2)}) async-start(s16[8,354,256]{2,1,0:T(8,128)(2,1)} %pad_add_fusion.6), calls=%async_computation.7 | async-start | bytes 2949120 | tf_op jit(solution)/shard_map/all_to_all | solution.py:62
  368.3 40.0 %all-to-all-start.6 = ((s16[8,354,256]{2,1,0:T(8,128)(2,1)}), s16[8,354,256]{2,1,0:T(8,128)(2,1)}, u32[]{:S(2)}, u32[]{:S(2)}) async-start(s16[8,354,256]{2,1,0:T(8,128)(2,1)} %pad_add_fusion.5), calls=%async_computation.6 | async-start | bytes 2949120 | tf_op jit(solution)/shard_map/all_to_all | solution.py:62
  425.8 6.3 %copy-start.1 = (bf16[1,1152,1408]{2,1,0:T(8,128)(2,1)S(1)}, bf16[1,1152,1408]{2,1,0:T(8,128)(2,1)}, u32[]{:S(2)}) copy-start(bf16[1,1152,1408]{2,1,0:T(8,128)(2,1)} %param.14) | copy-start | bytes 9732100
Sparse Core Ops, SparseCore 0:
  34.1 120.3 reduce-scatter.3
  325.7 62.6 all-gather.3
